TPU v7x, 32 devices: a whole 2x2x4 slice. The times are simulated.
32 devices in a mesh: groups: 2 (over y), view: 4 (over z), cuts: 2 (over x), row: 2 (over core).
Axes of the slice: x: 2, y: 2, z: 4, core: 2. Of those that a mesh axis runs over, the one named last changes fastest.
Arguments:
- sinogram: bfloat16 [4, 512, 2048], P('groups', ('view', 'cuts', 'row')), parts along dimension 0, may hold values from -1.5 to 1.5
- leaf_offsets: int32 [512, 512], P('view'), may hold values from 0 to 62
- leaf_frac: float32 [512, 512], P('view'), may hold values from 0 to 1
- merge_offsets: int32 [2, 4096], replicated, may hold values from 0 to 1020, as said below
- merge_weights: float32 [2, 4, 4096], replicated, may hold values from 0.1 to 0.6
Outputs:
- images: float32 [4, 2048, 2048], P(('groups', 'cuts'), ('view', 'row')), parts along dimension 0
There are 2 independent parts, one for each index of `groups`. A program takes and returns all parts, laid end to end along the dimension named above; an argument that names none is the same for every part. Nothing has to cross between parts.
Inputs may be any that keep to these rules, and one draw needn't show every extreme that they name: merge_offsets[l, j] + 4 <= 512 * 2^l.
All inputs are finite; a program needn't handle non-finite values.
Results may differ from a plain program's by a relative error of at most 0.0075.
Values may be sent and summed in bfloat16 or wider, within the bound.
A program may use at most 128 MiB of HBM per device.

v0:
```python
import math

import jax
import jax.numpy as jnp
from jax import lax
from jax.sharding import PartitionSpec as P

SHIFT = 32
TAPS = 4


def from_partner(block, axis, apart):
    count = lax.axis_size(axis)
    route = []
    for low in range(count):
        high = low | 1 << apart
        if high != low and high < count:
            route += [(low, high), (high, low)]
    return lax.ppermute(block, axis, route)


def ramp_matrix(length):
    positions = jnp.arange(length, dtype=jnp.int32)
    distance = positions[:, None] - positions[None, :]
    is_odd = jnp.abs(distance) % 2 == 1
    spacing = jnp.where(is_odd, distance, 1).astype(jnp.float32)
    entries = jnp.where(
        distance == 0, 0.25, jnp.where(is_odd, -1.0 / (math.pi * math.pi * spacing * spacing), 0.0)
    )
    return entries.astype(jnp.bfloat16)


def shifted_stack(filtered):
    length = filtered.shape[0]
    padded = jnp.pad(filtered, ((SHIFT, SHIFT), (0, 0)))
    copies = [padded[tap_number : tap_number + length] for tap_number in range(2 * SHIFT)]
    return jnp.concatenate(copies, axis=1)


def tap_kernel(offsets, fraction):
    tap_index = jnp.arange(2 * SHIFT, dtype=jnp.int32)[:, None, None]
    near_weight = (1.0 - fraction).astype(jnp.bfloat16)[None]
    far_weight = fraction.astype(jnp.bfloat16)[None]
    kernel = jnp.where(
        tap_index == offsets[None],
        near_weight,
        jnp.where(tap_index == offsets[None] + 1, far_weight, jnp.zeros((), jnp.bfloat16)),
    )
    return kernel.reshape(-1, offsets.shape[1])


def leaf_blocks(stacked, kernel, block_ids, block_rows):
    blocks = block_ids.shape[0]
    width = stacked.shape[1]
    chosen = jnp.take(stacked.reshape(-1, block_rows, width), block_ids, axis=0).reshape(
        blocks * block_rows, width
    )
    product = jnp.dot(chosen, kernel, preferred_element_type=jnp.float32)
    return product.reshape(blocks, block_rows, kernel.shape[1])


def resample(merge_offsets, merge_weights, depth, cohort, breadth):
    anchor = cohort * (2 * breadth)
    offsets = lax.dynamic_slice_in_dim(merge_offsets[depth], anchor, 2 * breadth, 0)
    weights = lax.dynamic_slice_in_dim(merge_weights[depth], anchor, 2 * breadth, 1)
    row_index = jnp.arange(breadth, dtype=jnp.int32)[:, None]
    running = jnp.zeros((breadth, 2 * breadth), jnp.float32)
    for tap_number in range(TAPS):
        running = running + jnp.where(
            row_index == offsets[None, :] + tap_number,
            weights[tap_number][None, :],
            jnp.zeros((), jnp.float32),
        )
    return running.astype(jnp.bfloat16)


def body(sinogram, leaf_offsets, leaf_frac, merge_offsets, merge_weights):
    cut_count = lax.axis_size("cuts")
    row_count = lax.axis_size("row")
    view_count = lax.axis_size("view")
    depths = view_count.bit_length() - 1
    row_member = lax.axis_index("row")
    view_member = lax.axis_index("view")
    image_side = sinogram.shape[2]
    block_rows = image_side // (2 * view_count)
    leaf_cols = image_side // view_count
    regrouped = lax.all_to_all(sinogram, "cuts", split_axis=0, concat_axis=1, tiled=True)
    readings = regrouped[0]
    own_views = readings.shape[0]
    filtered = lax.dot_general(
        ramp_matrix(image_side),
        readings,
        (((1,), (1,)), ((), ())),
        preferred_element_type=jnp.float32,
    ).astype(jnp.bfloat16)
    shaped_offsets = leaf_offsets.reshape(cut_count, row_count, -1, leaf_cols)
    shaped_fraction = leaf_frac.reshape(cut_count, row_count, -1, leaf_cols)
    mine_offsets = lax.dynamic_index_in_dim(shaped_offsets, row_member, 1, keepdims=False).reshape(
        own_views, leaf_cols
    )
    mine_fraction = lax.dynamic_index_in_dim(
        shaped_fraction, row_member, 1, keepdims=False
    ).reshape(own_views, leaf_cols)
    stacked = shifted_stack(filtered)
    kernel = tap_kernel(mine_offsets, mine_fraction)
    positions = jnp.arange(lax.axis_size("row") * view_count, dtype=jnp.int32)
    block_ids = 2 * (positions % view_count) + positions // view_count
    leaf_total = lax.psum_scatter(
        leaf_blocks(stacked, kernel, block_ids, block_rows), "row", scatter_dimension=0, tiled=True
    )
    current = leaf_total.astype(jnp.bfloat16)
    for depth in range(depths):
        breadth = leaf_cols << depth
        cohort = view_member >> depth
        parity = cohort % 2
        halves = current.reshape(-1, 2, block_rows, breadth)
        kept_rows = lax.dynamic_index_in_dim(halves, parity, 1, keepdims=False)
        sent_rows = lax.dynamic_index_in_dim(halves, 1 - parity, 1, keepdims=False)
        own_operator = resample(merge_offsets, merge_weights, depth, cohort, breadth)
        incoming = from_partner(sent_rows, "view", depth)
        other_operator = resample(
            merge_offsets, merge_weights, depth, cohort + 1 - 2 * parity, breadth
        )
        merged = jnp.dot(kept_rows, own_operator, preferred_element_type=jnp.float32) + jnp.dot(
            incoming, other_operator, preferred_element_type=jnp.float32
        )
        current = merged if depth == depths - 1 else merged.astype(jnp.bfloat16)
    return current


def solution(mesh):
    placed = (
        P("groups", ("view", "cuts", "row"), None),
        P("view", None),
        P("view", None),
        P(),
        P(),
    )
    return jax.shard_map(
        body,
        mesh=mesh,
        in_specs=placed,
        out_specs=P(("groups", "cuts"), ("view", "row"), None),
        check_vma=False,
    )
```

profile of v0, /device:TPU:9, one launch (start us, length us, event | category | flops | bytes accessed | tf_op | source)
XLA Modules:
  0.0 217.6 jit_solution(13458844031597850148)
XLA Ops:
  6.5 3.6 %all-to-all-start = ((bf16[2,32,2048]{2,1,0:T(8,128)(2,1)}), bf16[2,32,2048]{2,1,0:T(8,128)(2,1)S(1)}, u32[]{:S(2)}, u32[]{:S(2)}) async-start(bf16[2,32,2048]{2,1,0:T(8,128)(2,1)} %param.5), calls=%async_computation | async-start | bytes 524288 | tf_op jit(solution)/shard_map/all_to_all | solution.py:87
  10.2 0.9 subtract_convert_fusion
  11.1 0.9 dynamic-slice_convert_fusion
  12.2 3.6 %fusion.14 = bf16[4096,512]{1,0:T(8,128)(2,1)} fusion(s32[64,512]{1,0:T(8,128)S(1)} %broadcast_add_fusion, s32[64,512]{1,0:T(8,128)S(1)} %bitcast.85, s32[4096]{0:T(1024)S(1)} %eq.307, bf16[64,512]{1,0:T(8,128)(2,1)S(1)} %bitcast.87, bf16[64,512]{1,0:T(8,128)(2,1)S(1)} %bitcast.86), kind=kLoop, calls=%fused_computation.33 | loop fusion | flops 8388608 | bytes 4603904 | tf_op jit(solution)/shard_map/jit(_where)/select_n | solution.py:44
  15.8 15.2 %fusion.21 = bf16[2048,64]{0,1:T(8,128)(2,1)S(1)} fusion(bf16[64,2048]{1,0:T(8,128)(2,1)S(1)} %bitcast.88), kind=kOutput, calls=%fused_computation.40 | convolution fusion | flops 633470976 | bytes 524288 | tf_op jit(solution)/shard_map/dot_general | solution.py:90
  33.5 0.9 slice_dynamic-update-slice_fusion.59
  34.4 0.9 slice_dynamic-update-slice_fusion.58
  36.1 0.8 slice_dynamic-update-slice_fusion.56
  37.0 0.9 slice_dynamic-update-slice_fusion.55
  37.8 0.8 slice_dynamic-update-slice_fusion.54
  38.7 0.9 slice_dynamic-update-slice_fusion.53
  39.5 0.9 slice_dynamic-update-slice_fusion.52
  47.1 0.9 slice_dynamic-update-slice_fusion.43
  48.0 0.9 slice_dynamic-update-slice_fusion.42
  48.8 0.9 slice_dynamic-update-slice_fusion.41
  50.5 0.9 slice_dynamic-update-slice_fusion.39
  52.2 0.9 slice_dynamic-update-slice_fusion.37
  53.1 0.9 slice_dynamic-update-slice_fusion.36
  56.5 0.9 slice_dynamic-update-slice_fusion.32
  57.3 0.9 slice_dynamic-update-slice_fusion.31
  58.9 0.9 slice_dynamic-update-slice_fusion.30
  59.8 0.9 slice_dynamic-update-slice_fusion.29
  62.3 0.9 slice_dynamic-update-slice_fusion.26
  64.0 0.9 slice_dynamic-update-slice_fusion.24
  64.9 0.9 slice_dynamic-update-slice_fusion.23
  65.7 0.9 slice_dynamic-update-slice_fusion.22
  70.0 0.8 slice_dynamic-update-slice_fusion.17
  70.8 0.9 slice_dynamic-update-slice_fusion.16
  71.7 0.9 slice_dynamic-update-slice_fusion.15
  72.5 0.9 slice_dynamic-update-slice_fusion.14
  76.7 0.8 slice_dynamic-update-slice_fusion.9
  78.4 0.9 slice_dynamic-update-slice_fusion.7
  79.3 0.9 slice_dynamic-update-slice_fusion.6
  81.0 0.9 slice_dynamic-update-slice_fusion.4
  85.2 20.9 %copy.8 = bf16[2048,4096]{1,0:T(8,128)(2,1)} copy(bf16[2048,4096]{0,1:T(8,128)(2,1)} %slice_dynamic-update-slice_fusion) | data formatting | bytes 33554432 | tf_op jit(solution)/shard_map/reshape | solution.py:55
  106.1 11.8 %fusion.72 = (bf16[8,256,2048]{2,1,0:T(8,128)(2,1)}, bf16[8,256,2048]{2,1,0:T(8,128)(2,1)}) fusion(bf16[8,256,4096]{2,1,0:T(8,128)(2,1)} %bitcast.82), kind=kLoop, calls=%fused_computation.214 | loop fusion | bytes 33554432 | tf_op jit(solution)/shard_map/jit(_take)/gather | solution.py:55
  117.9 8.1 %gather_fusion = bf16[8,256,2048]{2,1,0:T(8,128)(2,1)} fusion(bf16[8,256,2048]{2,1,0:T(8,128)(2,1)} %get-tuple-element.13, s32[1024]{0:T(1024)S(1)} %pad_clamp_fusion), kind=kCustom, calls=%fused_computation | custom fusion | bytes 16777248 | tf_op jit(solution)/shard_map/jit(_take)/gather | solution.py:55
  126.0 8.1 %gather_fusion.1 = bf16[8,256,2048]{2,1,0:T(8,128)(2,1)} fusion(bf16[8,256,2048]{2,1,0:T(8,128)(2,1)} %get-tuple-element.14, s32[1024]{0:T(1024)S(1)} %pad_clamp_fusion), kind=kCustom, calls=%fused_computation.1 | custom fusion | bytes 16777248 | tf_op jit(solution)/shard_map/jit(_take)/gather | solution.py:55
  134.1 15.1 %fusion.5 = f32[8,256,512]{2,1,0:T(8,128)} fusion(bf16[8,256,2048]{2,1,0:T(8,128)(2,1)} %gather_fusion.1, bf16[8,256,2048]{2,1,0:T(8,128)(2,1)} %gather_fusion, pred[8]{0:T(512)(128)(4,1)S(1)} %compare_and_fusion, bf16[4096,512]{1,0:T(8,128)(2,1)} %fusion.14), kind=kOutput, calls=%fused_computation.12 | convolution fusion | flops 8631877632 | bytes 25165832 | tf_op jit(solution)/shard_map/dot_general | solution.py:58
  149.8 13.9 %reduce-scatter.2.cloned.1.call-done = f32[4,256,512]{2,1,0:T(8,128)} async-done(((f32[8,256,512]{2,1,0:T(8,128)}), f32[4,256,512]{2,1,0:T(8,128)}) %reduce-scatter.2.cloned.1.call-update) | async-done | bytes 2097168 | tf_op jit(solution)/shard_map/reduce_scatter | solution.py:108
  163.7 1.7 convert_element_type.56
  165.6 1.3 fusion.25
  166.9 11.8 %collective-permute-done = bf16[2,256,512]{2,1,0:T(8,128)(2,1)S(1)} collective-permute-done((bf16[2,256,512]{2,1,0:T(8,128)(2,1)S(1)}, bf16[2,256,512]{2,1,0:T(8,128)(2,1)S(1)}, u32[]{:S(2)}, u32[]{:S(2)}) %collective-permute-start) | collective-permute-done | bytes 524320 | tf_op jit(solution)/shard_map/ppermute | solution.py:19
  178.7 1.3 add_convert_fusion.8
  180.1 2.2 %collective-permute-start.1 = (bf16[1,256,1024]{2,1,0:T(8,128)(2,1)S(1)}, bf16[1,256,1024]{2,1,0:T(8,128)(2,1)S(1)}, u32[]{:S(2)}, u32[]{:S(2)}) collective-permute-start(bf16[1,256,1024]{2,1,0:T(8,128)(2,1)S(1)} %constant_dynamic-slice_fusion.14), channel_id=1, source_target_pairs={{0,8},{8,0},{4,12},{12,4},{1,9},{9,1},{5,13},{13,5},{2,10},{10,2},... | collective-permute-start | bytes 1572872 | tf_op jit(solution)/shard_map/ppermute | solution.py:19
  182.3 4.8 %fusion.17 = f32[256,2048]{1,0:T(8,128)S(1)} fusion(f32[2048]{0:T(1024)S(1)} %bitcast.104, s32[2048]{0:T(1024)S(1)} %bitcast.107, f32[2048]{0:T(1024)S(1)} %bitcast.101, s32[2048]{0:T(1024)S(1)} %bitcast.108, f32[2048]{0:T(1024)S(1)} %bitcast.102, s32[2048]{0:T(1024)S(1)} %bitcast.100, f32[2048]{0:T(1024)S(1)} %bitcast.103, s32[2048]{0:T(1024)S(1)} %bitcast.92, ...), kind=kOutput, calls=%fused_computation.36 | convolution fusion | flops 1098907648 | bytes 2686980 | tf_op jit(solution)/shard_map/dot_general | solution.py:124
  187.0 18.0 %collective-permute-done.1 = bf16[1,256,1024]{2,1,0:T(8,128)(2,1)S(1)} collective-permute-done((bf16[1,256,1024]{2,1,0:T(8,128)(2,1)S(1)}, bf16[1,256,1024]{2,1,0:T(8,128)(2,1)S(1)}, u32[]{:S(2)}, u32[]{:S(2)}) %collective-permute-start.1) | collective-permute-done | bytes 524320 | tf_op jit(solution)/shard_map/ppermute | solution.py:19
  205.1 5.6 %fusion.20 = f32[1,256,2048]{2,1,0:T(8,128)} fusion(f32[256,2048]{1,0:T(8,128)S(1)} %fusion.17, f32[2048]{0:T(1024)S(1)} %bitcast.99, s32[2048]{0:T(1024)S(1)} %bitcast.106, f32[2048]{0:T(1024)S(1)} %bitcast.97, s32[2048]{0:T(1024)S(1)} %bitcast.105, f32[2048]{0:T(1024)S(1)} %bitcast.98, s32[2048]{0:T(1024)S(1)} %bitcast.95, f32[2048]{0:T(1024)S(1)} %bitcast.96, ...), kind=kOutput, calls=%fused_computation.39 | convolution fusion | flops 1099431936 | bytes 4784128 | tf_op jit(solution)/shard_map/dot_general | solution.py:124
  (64 shorter events, 30.1 us)
Async XLA Ops:
  6.5 5.5 %copy-start = (s32[128,512]{1,0:T(8,128)S(1)}, s32[128,512]{1,0:T(8,128)}, u32[]{:S(2)}) copy-start(s32[128,512]{1,0:T(8,128)} %param.6) | copy-start | bytes 786436
  6.5 9.3 %all-to-all-start = ((bf16[2,32,2048]{2,1,0:T(8,128)(2,1)}), bf16[2,32,2048]{2,1,0:T(8,128)(2,1)S(1)}, u32[]{:S(2)}, u32[]{:S(2)}) async-start(bf16[2,32,2048]{2,1,0:T(8,128)(2,1)} %param.5), calls=%async_computation | async-start | bytes 524288 | tf_op jit(solution)/shard_map/all_to_all | solution.py:87
  10.1 153.6 %reduce-scatter.2.cloned.1.call-start = ((), (), s32[]{:S(2)}) async-start(), calls=%async_computation.2 | async-start | bytes 6291456 | tf_op jit(solution)/shard_map/reduce_scatter | solution.py:108
  134.1 15.2 %copy-start.3 = (s32[2,4096]{1,0:T(2,128)S(1)}, s32[2,4096]{1,0:T(2,128)}, u32[]{:S(2)}) copy-start(s32[2,4096]{1,0:T(2,128)} %param.8) | copy-start | bytes 98308
  134.1 15.3 %copy-start.2 = (f32[2,4,4096]{2,1,0:T(4,128)S(1)}, f32[2,4,4096]{2,1,0:T(4,128)}, u32[]{:S(2)}) copy-start(f32[2,4,4096]{2,1,0:T(4,128)} %param.9) | copy-start | bytes 393220
  165.5 13.2 %collective-permute-start = (bf16[2,256,512]{2,1,0:T(8,128)(2,1)S(1)}, bf16[2,256,512]{2,1,0:T(8,128)(2,1)S(1)}, u32[]{:S(2)}, u32[]{:S(2)}) collective-permute-start(bf16[2,256,512]{2,1,0:T(8,128)(2,1)S(1)} %dynamic-slice_bitcast_fusion), channel_id=1, source_target_pairs={{0,4},{4,0},{8,12},{12,8},{1,5},{5,1},{9,13},{13,9},{2,6},{6,2},{1... | collective-permute-start | bytes 1572872 | tf_op jit(solution)/shard_map/ppermute | solution.py:19
  180.1 25.0 %collective-permute-start.1 = (bf16[1,256,1024]{2,1,0:T(8,128)(2,1)S(1)}, bf16[1,256,1024]{2,1,0:T(8,128)(2,1)S(1)}, u32[]{:S(2)}, u32[]{:S(2)}) collective-permute-start(bf16[1,256,1024]{2,1,0:T(8,128)(2,1)S(1)} %constant_dynamic-slice_fusion.14), channel_id=1, source_target_pairs={{0,8},{8,0},{4,12},{12,4},{1,9},{9,1},{5,13},{13,5},{2,10},{10,2},... | collective-permute-start | bytes 1572872 | tf_op jit(solution)/shard_map/ppermute | solution.py:19
  205.1 5.6 %copy-start.1 = (s32[128,512]{1,0:T(8,128)S(1)}, s32[128,512]{1,0:T(8,128)}, u32[]{:S(2)}) copy-start(s32[128,512]{1,0:T(8,128)} %param.6) | copy-start | bytes 786436
Sparse Core Ops, SparseCore 0:
  149.3 14.3 reduce-scatter.1
where the time goes:
time: 221 us; the launch traced here: 218 us
  local copies, waits for them, and re-layouts  104 us (47%)
  waiting for transfers between devices  43.7 us (20%)
  matrix products  43.3 us (20%)
  between operations  13.7 us (6%)
  other arithmetic  6.41 us (3%)
  starting transfers between devices  5.96 us (3%)
    unnamed x71, local copies, waits for them, and re-layouts  53.3 us
    ppermute x2, waiting for transfers between devices, from_partner(): return lax.ppermute(block, axis, route)  29.8 us
    gather x3, local copies, waits for them, and re-layouts, leaf_blocks(): jnp.take(stacked.reshape(-1, block_rows, width), block_ids, axis=0)  28 us
    reshape x1, local copies, waits for them, and re-layouts, leaf_blocks(): stacked.reshape(-1, block_rows, width)  20.9 us
    dot_general x1, matrix products, body(): lax.dot_general(ramp_matrix(image_side), readings, (((1,), (1,)), ((), ()...  15.2 us
    dot_general x1, matrix products, leaf_blocks(): product = jnp.dot(chosen, kernel, preferred_element_type=jnp.float32)  15.1 us
    reduce_scatter x1, waiting for transfers between devices, body(): lax.psum_scatter(leaf_blocks(stacked, kernel, block_ids, block_rows), 'ro...  13.9 us
    dot_general x2, matrix products, body(): jnp.dot(incoming, other_operator, preferred_element_type=jnp.float32)  6.96 us
  transfers between devices with their start and end apart: 4, of which 3 were waited for; matrix products, arithmetic and copies ran while one was open for 6% of the time, Pallas kernels for 0%

commit v1 on v0

v1 whole, which is shorter than its diff:
```python
import functools
import math

import jax
import jax.numpy as jnp
import numpy as np
from jax import lax
from jax.experimental import pallas as pl
from jax.experimental.pallas import tpu as pltpu
from jax.sharding import PartitionSpec as P

SHIFT = 32
TAPS = 4
SPAN = 2 * SHIFT
STEP = 16
MESH = pl.DeviceIdType.MESH


def ramp_band(length, block, window):
    blocks = length // block
    rows = np.arange((2 * blocks - 1) * block)[:, None] - (blocks - 1) * block
    apart = rows + SHIFT - np.arange(window)[None, :]
    odd = np.abs(apart) % 2 == 1
    spacing = np.where(odd, apart, 1).astype(np.float32)
    entries = np.where(
        apart == 0, 0.25, np.where(odd, -1.0 / (math.pi * math.pi * spacing * spacing), 0.0)
    )
    return entries.astype(np.float32).astype(jnp.bfloat16)


def kernel(
    dims,
    sino, offs, frac, moffs, mweights, band_hbm,
    out,
    band, stage, filt, tab, tall, shifted, taps, subs, maps,
    band_sem, send_f, recv_f, send_t, recv_t, send_p, recv_p,
):
    views, cuts, rows, planes, slices, own, length, block, window, per, cols, levels = dims
    group = lax.axis_index("groups")
    view = lax.axis_index("view")
    cut = lax.axis_index("cuts")
    row = lax.axis_index("row")
    members = views * cuts * rows
    sources = cuts * rows
    me = (view * cuts + cut) * rows + row
    part = group * rows + row
    share = per // planes
    bf16 = jnp.bfloat16
    f32 = jnp.float32

    load_band = pltpu.make_async_copy(band_hbm, band, band_sem)
    load_band.start()

    def member_id(d):
        return {"view": d // (cuts * rows), "cuts": (d // rows) % cuts, "row": d % rows}

    def plane_id(p):
        return {"groups": p // rows, "row": p % rows}

    barrier = pltpu.get_barrier_semaphore()

    @pl.loop(1, members)
    def _(k):
        pl.semaphore_signal(
            barrier, inc=1, device_id=member_id((me + k) % members), device_id_type=MESH
        )

    away = planes // rows - 1
    for g in range(1, away + 1):
        for r in range(rows):
            pl.semaphore_signal(
                barrier,
                inc=1,
                device_id={"groups": (group + g) % (away + 1), "row": r},
                device_id_type=MESH,
            )

    for p in range(planes):
        span = pl.ds(p * share, share)
        tab[view, p, 0] = offs[span, :].astype(f32).astype(bf16)
        tab[view, p, 1] = (frac[span, :] - 0.5).astype(bf16)

    pl.semaphore_wait(barrier, members - 1 + away * rows)

    def table_copy(k):
        return pltpu.make_async_remote_copy(
            src_ref=tab.at[view, part],
            dst_ref=tab.at[view, part],
            send_sem=send_t.at[k],
            recv_sem=recv_t.at[view],
            device_id={"view": (view + k) % views},
            device_id_type=MESH,
        )

    @pl.loop(1, views)
    def _(k):
        table_copy(k).start()

    load_band.wait()
    readings = sino[...].astype(f32).reshape(slices * own, length).astype(bf16)
    lane = lax.broadcasted_iota(jnp.int32, (slices * own, window), 1)
    blocks = length // block

    @pl.loop(0, blocks)
    def _(w):
        start = pl.multiple_of((blocks - 1 - w) * block, block)
        value = jnp.dot(readings, band[pl.ds(start, length), :], preferred_element_type=f32)
        place = lane + (w * block - SHIFT)
        value = jnp.where((place >= 0) & (place < length), value, 0.0)
        for s in range(slices):
            stage[((w // rows) * cuts + s) * rows + w % rows] = value[
                s * own : (s + 1) * own
            ].astype(bf16)

    def filtered_copy(k):
        d = (me + k) % members
        return pltpu.make_async_remote_copy(
            src_ref=stage.at[d],
            dst_ref=filt.at[me],
            send_sem=send_f.at[d],
            recv_sem=recv_f.at[me],
            device_id=member_id(d),
            device_id_type=MESH,
        )

    @pl.loop(1, members)
    def _(k):
        filtered_copy(k).start()

    filt[me] = stage[me]

    for level in range(levels):
        width = cols << level
        tile = min(width, 256)
        index = lax.broadcasted_iota(jnp.int32, (tile, tile), 0).astype(f32).astype(bf16)
        count = views >> level
        tiles = 2 * width // tile

        @pl.loop(0, count * tiles)
        def _(i):
            g = i // tiles
            column = pl.multiple_of((i % tiles) * tile, tile)
            at = pl.ds(pl.multiple_of(i * tile, tile), tile)
            offset = moffs[level : level + 1, at].astype(f32)
            weights = [mweights[level, k : k + 1, at].astype(bf16) for k in range(TAPS)]
            for b in range(width // tile):
                near = jnp.clip(offset - float(b * tile), -8.0, float(tile + 8)).astype(bf16)
                apart = index - near
                entry = jnp.zeros((tile, tile), bf16)
                for k in range(TAPS):
                    entry = jnp.where(apart == jnp.asarray(k, bf16), weights[k], entry)
                down = pl.multiple_of((g % 2) * width + b * tile, tile)
                maps[level][g // 2, pl.ds(down, tile), pl.ds(column, tile)] = entry

    def plane_copy(k, m):
        v = (view + k) % views
        return pltpu.make_async_remote_copy(
            src_ref=tab.at[v, part],
            dst_ref=tab.at[v, part],
            send_sem=send_p.at[k, m],
            recv_sem=recv_p.at[v, part],
            device_id=plane_id((part + m) % planes),
            device_id_type=MESH,
        )

    def table_arrival(v, p, sem):
        return pltpu.make_async_remote_copy(
            src_ref=tab.at[v, p],
            dst_ref=tab.at[v, p],
            send_sem=send_t.at[0],
            recv_sem=sem,
            device_id={"view": view},
            device_id_type=MESH,
        )

    @pl.loop(1, views)
    def _(k):
        v = (view + k) % views
        table_arrival(v, part, recv_t.at[v]).wait_recv()
        for m in range(1, planes):
            plane_copy(k, m).start()

    def filtered_arrival(d):
        return pltpu.make_async_remote_copy(
            src_ref=filt.at[d],
            dst_ref=filt.at[d],
            send_sem=send_t.at[0],
            recv_sem=recv_f.at[d],
            device_id={"view": view},
            device_id_type=MESH,
        )

    @pl.loop(0, views)
    def _(k):
        v = (view + k) % views

        @pl.loop(0, sources)
        def _(i):
            d = v * sources + i

            @pl.when(d != me)
            def _():
                filtered_arrival(d).wait_recv()

        @pl.when(k > 0)
        def _():
            for m in range(1, planes):
                p = (part + m) % planes
                table_arrival(v, p, recv_p.at[v, p]).wait_recv()

        rays = filt[pl.ds(v * sources, sources)].astype(f32).reshape(per, window)
        tall[...] = rays.T
        reach = block + SPAN - STEP
        for b in range(STEP):
            shifted[:, b * per : (b + 1) * per] = tall[pl.ds(b, reach), :].astype(bf16)

        tight = min(share, STEP)
        inner = share // tight

        @pl.loop(0, per // tight)
        def _(i):
            span = pl.ds(pl.multiple_of((i % inner) * tight, tight), tight)
            where = tab[v, i // inner, 0, span, :]
            frac_off = tab[v, i // inner, 1, span, :].astype(f32)
            near = (0.5 - frac_off).astype(bf16)
            far = (0.5 + frac_off).astype(bf16)
            zero = jnp.zeros((tight, cols), bf16)
            before = None
            for t in range(SPAN):
                here = where == jnp.asarray(t, bf16)
                entry = zero if before is None else jnp.where(before, far, zero)
                entry = jnp.where(here, near, entry)
                before = here
                down = pl.multiple_of((t % STEP) * per + i * tight, tight)
                taps[t // STEP, pl.ds(down, tight), :] = entry

        total = jnp.zeros((block, cols), f32)
        for a in range(SPAN // STEP):
            total = total + jnp.dot(
                shifted[a * STEP : a * STEP + block, :], taps[a], preferred_element_type=f32
            )
        across = pl.multiple_of((v % 2) * cols, cols)
        subs[0][v // 2, :, pl.ds(across, cols)] = total.astype(bf16)

    for level in range(levels):
        width = cols << level
        tile = min(2 * width, 512)
        tiles = 2 * width // tile
        pairs = views >> (level + 1)
        last = level == levels - 1

        @pl.loop(0, pairs * tiles)
        def _(i):
            g = i // tiles
            column = pl.multiple_of((i % tiles) * tile, tile)
            merged = jnp.dot(
                subs[level][g], maps[level][g, :, pl.ds(column, tile)], preferred_element_type=f32
            )
            if last:
                out[0, :, pl.ds(column, tile)] = merged
            else:
                across = pl.multiple_of((g % 2) * 2 * width + column, tile)
                subs[level + 1][g // 2, :, pl.ds(across, tile)] = merged.astype(bf16)

    @pl.loop(1, members)
    def _(k):
        filtered_copy(k).wait_send()

    @pl.loop(1, views)
    def _(k):
        table_copy(k).wait_send()
        for m in range(1, planes):
            plane_copy(k, m).wait_send()


def body(sinogram, leaf_offsets, leaf_frac, merge_offsets, merge_weights):
    cuts = lax.axis_size("cuts")
    rows = lax.axis_size("row")
    views = lax.axis_size("view")
    planes = lax.axis_size("groups") * rows
    levels = views.bit_length() - 1
    slices, own, length = sinogram.shape
    per, cols = leaf_offsets.shape
    block = length // (rows * views)
    window = -(-(block + SPAN) // 128) * 128
    members = views * cuts * rows
    dims = (views, cuts, rows, planes, slices, own, length, block, window, per, cols, levels)
    band = jnp.asarray(ramp_band(length, block, window))
    vmem = pl.BlockSpec(memory_space=pltpu.VMEM)
    bf16 = jnp.bfloat16
    dma = pltpu.SemaphoreType.DMA
    return pl.pallas_call(
        functools.partial(kernel, dims),
        out_shape=jax.ShapeDtypeStruct((1, block, length), jnp.float32),
        in_specs=[vmem] * 5 + [pl.BlockSpec(memory_space=pl.ANY)],
        out_specs=vmem,
        scratch_shapes=[
            pltpu.VMEM(band.shape, bf16),
            pltpu.VMEM((members, own, window), bf16),
            pltpu.VMEM((members, own, window), bf16),
            pltpu.VMEM((views, planes, 2, per // planes, cols), bf16),
            pltpu.VMEM((window, per), jnp.float32),
            pltpu.VMEM((block + SPAN - STEP, STEP * per), bf16),
            pltpu.VMEM((SPAN // STEP, STEP * per, cols), bf16),
            [pltpu.VMEM((views >> (n + 1), block, cols << (n + 1)), bf16) for n in range(levels)],
            [
                pltpu.VMEM((views >> (n + 1), cols << (n + 1), cols << (n + 1)), bf16)
                for n in range(levels)
            ],
            dma,
            dma((members,)),
            dma((members,)),
            dma((views,)),
            dma((views,)),
            dma((views, planes)),
            dma((views, planes)),
        ],
        compiler_params=pltpu.CompilerParams(
            collective_id=0, has_side_effects=True, vmem_limit_bytes=60 * 1024 * 1024
        ),
    )(sinogram, leaf_offsets, leaf_frac, merge_offsets, merge_weights, band)


def solution(mesh):
    placed = (
        P("groups", ("view", "cuts", "row"), None),
        P("view", None),
        P("view", None),
        P(),
        P(),
    )
    return jax.shard_map(
        body,
        mesh=mesh,
        in_specs=placed,
        out_specs=P(("groups", "cuts"), ("view", "row"), None),
        check_vma=False,
    )
```

time: 221 us -> 44 us (0.20); the launches traced: 218 us -> 43.8 us
  local copies, waits for them, and re-layouts: 104 us -> 3.14 us
  waiting for transfers between devices: 43.7 us -> 0 us
  matrix products: 43.3 us -> 0 us
  Pallas kernels: 0 us -> 40.7 us
  between operations: 13.7 us -> 0.01 us
  other arithmetic: 6.41 us -> 0 us
  starting transfers between devices: 5.96 us -> 0 us
    unnamed x71 -> x1, local copies, waits for them, and re-layouts: 53.3 us -> 3.14 us
    dot_general x6 -> x0, matrix products: 43.3 us -> none  [the longest x1 15.2 us: body(): lax.dot_general(ramp_matrix(image_side), readings, (((1,), (1,)), ((), ()...]
    pallas_call x0 -> x1, Pallas kernels: none -> 40.7 us  [body(): pl.pallas_call(functools.partial(kernel, dims), out_shape=jax.ShapeDtypeS...]
    ppermute x2 -> x0, waiting for transfers between devices: 29.8 us -> none  [from_partner(): return lax.ppermute(block, axis, route)]
    gather x3 -> x0, local copies, waits for them, and re-layouts: 28 us -> none  [leaf_blocks(): jnp.take(stacked.reshape(-1, block_rows, width), block_ids, axis=0)]
    reshape x1 -> x0, local copies, waits for them, and re-layouts: 20.9 us -> none  [leaf_blocks(): stacked.reshape(-1, block_rows, width)]
    reduce_scatter x1 -> x0, waiting for transfers between devices: 13.9 us -> none  [body(): lax.psum_scatter(leaf_blocks(stacked, kernel, block_ids, block_rows), 'ro...]
    select_n x2 -> x0, other arithmetic: 3.65 us -> none  [the longest x1 3.64 us: tap_kernel(): jnp.where(tap_index == offsets[None], near_weight, jnp.where(tap_index ==...]
  transfers between devices with their start and end apart: 4 -> 0, of which waited for: 3 -> 0; matrix products, arithmetic and copies ran while one was open for 6% -> 0% of each run, Pallas kernels for 0% -> 0%
where the time goes in v1:
time: 44 us; the launch traced here: 43.8 us
  Pallas kernels  40.7 us (93%)
  local copies, waits for them, and re-layouts  3.14 us (7%)
    pallas_call x1, Pallas kernels, body(): pl.pallas_call(functools.partial(kernel, dims), out_shape=jax.ShapeDtypeS...  40.7 us
    unnamed x1, local copies, waits for them, and re-layouts  3.14 us

profile of v1, /device:TPU:9, one launch (start us, length us, event | category | flops | bytes accessed | tf_op | source)
XLA Modules:
  0.0 43.8 jit_solution(15275869554737225621)
XLA Ops:
  0.0 40.7 %shard_map.64 = f32[1,256,2048]{2,1,0:T(8,128)} custom-call(bf16[2,32,2048]{2,1,0:T(8,128)(2,1)} %sino.1, s32[128,512]{1,0:T(8,128)} %offs.1, f32[128,512]{1,0:T(8,128)} %frac.1, s32[2,4096]{1,0:T(2,128)} %moffs.1, f32[2,4,4096]{2,1,0:T(4,128)} %mweights.1, bf16[3840,384]{1,0:T(8,128)(2,1)} %constant.2.clone.band_hbm), custom_call_target="tpu_custom_call" | custom-call | tf_op jit(solution)/shard_map/pallas_call | solution.py:292
  40.7 3.1 %copy.8 = f32[1,256,2048]{2,1,0:T(8,128)} copy(f32[1,256,2048]{2,1,0:T(8,128)} %shard_map.64) | data formatting | bytes 4194304
